TPU v7x, 32 devices: a whole 2x2x4 slice. The times are simulated.
32 devices in a mesh: rot: 8 (over z, y), cls: 4 (over x, core).
Axes of the slice: x: 2, y: 2, z: 4, core: 2. Of those that a mesh axis runs over, the one named last changes fastest.
Arguments:
- particles: bfloat16 [128, 16384], P('rot'), may hold values from -64 to 64
- references: bfloat16 [48, 96, 16384], P('cls', 'rot'), may hold values from -0.046875 to 0.046875
- micrograph: int32 [8, 16], P('rot'), may hold values from 0 to 3, never falling along the last dimension, each value on 1 to 8 neighbouring positions
- ctf: float32 [32, 64], P('rot'), may hold values from -1 to 1
- prior_class: int32 [128], P('rot'), may hold values from 0 to 47
Outputs:
- class_scores: float32 [128, 48], P('rot', 'cls')
- best_score: float32 [128], P('rot')
- prior_score: float32 [128], P('rot')
Inputs may be any that keep to these rules, and one draw needn't show every extreme that they name: The entries of one row are the micrograph numbers of that index of rot in order, never falling; each of the 4 micrographs has 1 to 8 particles.
All inputs are finite; a program needn't handle non-finite values.
Results may differ from a plain program's by a relative error of at most 0.00095.
Values may be sent and summed in bfloat16 or wider, within the bound.
A program may use at most 128 MiB of HBM per device.

v0:
```python
import jax
import jax.numpy as jnp
from jax import lax
from jax.sharding import PartitionSpec as P

CYCLES = 64
POLAR = 128


def body(particles, references, micrograph, ctf, prior_class):
    part_count = particles.shape[0]
    micro_count = ctf.shape[0]
    class_count = references.shape[0]
    angle_count = references.shape[1]
    features = particles.shape[1]
    rotation_count = lax.axis_size("rot")
    particle_spectra = particles.astype(jnp.float32).reshape(part_count, CYCLES, 2 * POLAR)
    rotation_energy = jnp.mean(particle_spectra * particle_spectra, axis=2)
    indicator_matrix = (
        micrograph[0][:, None] == jnp.arange(micro_count, dtype=jnp.int32)[None, :]
    ).astype(jnp.float32)
    score_totals = jnp.dot(indicator_matrix.T, rotation_energy, precision=lax.Precision.HIGHEST)
    counts = jnp.sum(indicator_matrix, axis=0)
    mean_power = score_totals / counts[:, None]
    scaling_coefficient = ctf * lax.rsqrt(mean_power + 1e-06)
    particle_scores = jnp.dot(
        indicator_matrix, scaling_coefficient, precision=lax.Precision.HIGHEST
    )
    whitened = (
        (particle_spectra * particle_scores[:, :, None])
        .reshape(part_count, features)
        .astype(jnp.bfloat16)
    )
    ref_table = references.reshape(class_count * angle_count, features)
    portion = lax.all_gather(whitened, "rot", axis=0, tiled=True)
    scored = lax.dot_general(
        ref_table, portion, (((1,), (1,)), ((), ())), preferred_element_type=jnp.float32
    )
    best_local = jnp.max(scored.reshape(class_count, angle_count, portion.shape[0]), axis=1)
    blocks = best_local.reshape(class_count, rotation_count, part_count)
    received = lax.all_to_all(blocks, "rot", split_axis=1, concat_axis=1, tiled=True)
    owned = jnp.max(received, axis=1)
    class_scores = owned.T
    local_best = jnp.max(class_scores, axis=1)
    class_index = lax.axis_index("cls") * class_count + jnp.arange(class_count, dtype=jnp.int32)
    chosen = prior_class[:, None] == class_index[None, :]
    local_prior = jnp.max(jnp.where(chosen, class_scores, -1e30), axis=1)
    best_score, prior_score = lax.pmax((local_best, local_prior), "cls")
    return (class_scores, best_score, prior_score)


def solution(mesh):
    in_specs = (P("rot", None), P("cls", "rot", None), P("rot", None), P("rot", None), P("rot"))
    out_specs = (P("rot", "cls"), P("rot"), P("rot"))
    return jax.shard_map(body, mesh=mesh, in_specs=in_specs, out_specs=out_specs, check_vma=False)
```

profile of v0, /device:TPU:0, one launch (start us, length us, event | category | flops | bytes accessed | tf_op | source)
XLA Modules:
  0.0 118.3 jit_solution(16492835034037239104)
XLA Ops:
  7.2 0.0 copy-start.2
  7.2 0.0 copy-start
  7.2 0.0 copy-start.3
  7.2 0.0 all-gather.2.cloned.1.call-start
  7.2 0.8 convert_reduce_fusion
  8.1 1.1 convert_multiply_fusion.1
  9.2 0.3 copy.13
  9.5 0.2 reduce_sum.18
  9.7 0.0 copy-done.2
  9.7 0.0 copy-done.3
  9.7 0.1 fusion.2
  9.9 0.2 fusion.6
  10.1 0.2 mul.26
  10.3 0.6 copy.14
  10.9 0.0 copy-done
  10.9 1.0 fusion.3
  11.9 0.0 all-gather.2.cloned.1.call-update
  11.9 6.7 %reshape.27 = bf16[144,16384]{1,0:T(8,128)(2,1)} reshape(bf16[12,12,16384]{2,1,0:T(8,128)(2,1)} %param.6) | data formatting | bytes 9437184 | tf_op jit(solution)/shard_map/reshape | solution.py:34
  18.6 0.0 copy-start.1
  18.6 68.9 %all-gather.2.cloned.1.call-done = bf16[128,16384]{1,0:T(8,128)(2,1)} async-done(((bf16[16,16384]{1,0:T(8,128)(2,1)}), bf16[128,16384]{1,0:T(8,128)(2,1)}) %all-gather.2.cloned.1.call-update) | async-done | bytes 4194320 | tf_op jit(solution)/shard_map/all_gather | solution.py:35
  87.6 5.0 %convolution_bitcast_fusion = f32[144,128]{1,0:T(8,128)S(1)} fusion(bf16[128,16384]{1,0:T(8,128)(2,1)} %all-gather.2.cloned.1.call-done, bf16[144,16384]{1,0:T(8,128)(2,1)} %reshape.27), kind=kOutput, calls=%fused_computation.2 | convolution fusion | flops 603979776 | bytes 8986624 | tf_op jit(solution)/shard_map/dot_general | solution.py:36
  92.6 0.1 reshape.29
  92.7 0.7 reshape.30
  93.4 3.3 %all-to-all-start = ((f32[8,1,192]{2,1,0:T(1,128)}), f32[8,1,192]{2,1,0:T(1,128)S(1)}, u32[]{:S(2)}, u32[]{:S(2)}) async-start(f32[8,1,192]{2,1,0:T(1,128)} %reshape.30), calls=%async_computation | async-start | bytes 16384 | tf_op jit(solution)/shard_map/all_to_all | solution.py:41
  96.8 6.4 %all-to-all-done = f32[8,1,192]{2,1,0:T(1,128)S(1)} async-done(((f32[8,1,192]{2,1,0:T(1,128)}), f32[8,1,192]{2,1,0:T(1,128)S(1)}, u32[]{:S(2)}, u32[]{:S(2)}) %all-to-all-start) | async-done | bytes 6176 | tf_op jit(solution)/shard_map/all_to_all | solution.py:41
  103.2 0.5 broadcast.9
  103.7 0.7 reduce.2
  104.4 0.1 reshape.31
  104.5 0.7 copy.12
  105.2 0.0 copy-done.1
  105.2 0.1 select_reduce_fusion
  105.3 6.2 %all-reduce = (f32[16]{0:T(128)}, f32[16]{0:T(128)}) all-reduce(f32[16]{0:T(128)S(1)} %get-tuple-element.9, f32[16]{0:T(128)S(1)} %select_reduce_fusion), channel_id=1, replica_groups=mesh['rot'=8,'cls'=4] {'cls'}, use_global_device_ids=true, to_apply=%region_5.6 | all-reduce | flops 32 | bytes 256 | tf_op jit(solution)/shard_map/pmax | solution.py:48
  (5 shorter events, 0.1 us)
Async XLA Ops:
  7.2 2.6 %copy-start.2 = (s32[1,16]{1,0:T(1,128)S(1)}, s32[1,16]{1,0:T(1,128)}, u32[]{:S(2)}) copy-start(s32[1,16]{1,0:T(1,128)} %param.7) | copy-start | bytes 196
  7.2 3.7 %copy-start = (bf16[16,16384]{1,0:T(8,128)(2,1)S(1)}, bf16[16,16384]{1,0:T(8,128)(2,1)}, u32[]{:S(2)}) copy-start(bf16[16,16384]{1,0:T(8,128)(2,1)} %param.5) | copy-start | bytes 1572868
  7.2 2.5 %copy-start.3 = (f32[4,64]{1,0:T(4,128)S(1)}, f32[4,64]{1,0:T(4,128)}, u32[]{:S(2)}) copy-start(f32[4,64]{1,0:T(4,128)} %param.8) | copy-start | bytes 3076
  7.2 80.4 %all-gather.2.cloned.1.call-start = ((), (), s32[]{:S(2)}) async-start(), calls=%async_computation.1 | async-start | bytes 4718592 | tf_op jit(solution)/shard_map/all_gather | solution.py:35
  18.6 86.6 %copy-start.1 = (s32[16]{0:T(128)S(1)}, s32[16]{0:T(128)}, u32[]{:S(2)}) copy-start(s32[16]{0:T(128)} %param.9) | copy-start | bytes 196
  93.4 9.8 %all-to-all-start = ((f32[8,1,192]{2,1,0:T(1,128)}), f32[8,1,192]{2,1,0:T(1,128)S(1)}, u32[]{:S(2)}, u32[]{:S(2)}) async-start(f32[8,1,192]{2,1,0:T(1,128)} %reshape.30), calls=%async_computation | async-start | bytes 16384 | tf_op jit(solution)/shard_map/all_to_all | solution.py:41
Sparse Core Ops, SparseCore 0:
  12.0 75.5 all-gather.1
where the time goes:
time: 119 us; the launch traced here: 118 us
  waiting for transfers between devices  75.4 us (63%)
  between operations  14.2 us (12%)
  local copies, waits for them, and re-layouts  9.95 us (8%)
  blocking collectives  6.17 us (5%)
  matrix products  5.32 us (4%)
  other arithmetic  3.92 us (3%)
  starting transfers between devices  3.37 us (3%)
    all_gather x1, waiting for transfers between devices, body(): portion = lax.all_gather(whitened, 'rot', axis=0, tiled=True)  68.9 us
    reshape x1, local copies, waits for them, and re-layouts, body(): ref_table = references.reshape(class_count * angle_count, features)  6.73 us
    all_to_all x1, waiting for transfers between devices, body(): lax.all_to_all(blocks, 'rot', split_axis=1, concat_axis=1, tiled=True)  6.45 us
    pmax x1, blocking collectives, body(): best_score, prior_score = lax.pmax((local_best, local_prior), 'cls')  6.17 us
    dot_general x1, matrix products, body(): lax.dot_general(ref_table, portion, (((1,), (1,)), ((), ())), preferred_e...  5 us
    all_to_all x1, starting transfers between devices, body(): lax.all_to_all(blocks, 'rot', split_axis=1, concat_axis=1, tiled=True)  3.33 us
    unnamed x13, local copies, waits for them, and re-layouts  2.4 us
  transfers between devices with their start and end apart: 2, of which 2 were waited for; matrix products, arithmetic and copies ran while one was open for 6% of the time, Pallas kernels for 0%

commit v1 on v0

v1 whole, which is shorter than its diff:
```python
import functools
import jax
import jax.numpy as jnp
from jax import lax
from jax.experimental import pallas as pl
from jax.experimental.pallas import tpu as pltpu
from jax.sharding import PartitionSpec as P

CYCLES = 64
LOW = -1e30
VMEM_BYTES = 62 * 1024 * 1024


def plan(n_rot, n_cls):
    ys = 2 if n_rot % 2 == 0 else 1
    cs = 2 if n_cls % 2 == 0 else 1
    units = max(1, 64 // n_rot)
    crossing = (3 * units) // 8 if n_cls == 2 * cs else 0
    return n_rot // ys, ys, n_cls // cs, cs, units, crossing


def kernel(n_rot, n_cls, part_ref, ref_ref, mic_ref, ctf_ref, prior_ref,
           cls_out, best_out, prior_out,
           g, refs_v, refs_p, acc, fac, fac_t, cs_tx, cs_rx, bp,
           own_sem, ref_sem, recv_sem, send_sem, fac_send, fac_recv,
           sc_send, sc_recv, bp_send, bp_recv):
    zs, ys, xs, cores, units, crossing = plan(n_rot, n_cls)
    through = units - crossing
    parts, feats = part_ref.shape
    classes, angles, _ = ref_ref.shape
    width = feats // (cores * units)
    step = feats // CYCLES
    rot = lax.axis_index("rot")
    cls = lax.axis_index("cls")
    z, y = lax.div(rot, ys), lax.rem(rot, ys)
    x, core = lax.div(cls, cores), lax.rem(cls, cores)

    own = pltpu.make_async_copy(part_ref, g.at[rot], own_sem)
    own.start()
    ref_copies = [
        pltpu.make_async_copy(ref_ref.at[c], refs_v.at[c], ref_sem.at[c]) for c in range(classes)
    ]
    for copy in ref_copies:
        copy.start()

    barrier = pltpu.get_barrier_semaphore()
    for d in range(1, n_rot):
        pl.semaphore_signal(barrier, inc=1, device_id=(lax.rem(rot + d, n_rot), cls),
                            device_id_type=pl.DeviceIdType.MESH)
    for d in range(1, n_cls):
        pl.semaphore_signal(barrier, inc=1, device_id=(rot, lax.rem(cls + d, n_cls)),
                            device_id_type=pl.DeviceIdType.MESH)
    pl.semaphore_wait(barrier, n_rot + n_cls - 2)

    def unit_of(j):
        return jnp.where(x == 0, j, units - 1 - j) if crossing else j

    def piece(shard, unit, half, dev, kind):
        col = pl.multiple_of((half * units + unit) * width, 128)
        ref = g.at[shard, :, pl.ds(col, width)]
        return pltpu.make_async_remote_copy(
            src_ref=ref, dst_ref=ref,
            send_sem=send_sem.at[kind, shard, unit],
            recv_sem=recv_sem.at[shard, half * units + unit],
            device_id=dev, device_id_type=pl.DeviceIdType.MESH)

    up, down = ((z + 1) * ys + y, cls), ((z - 1) * ys + y, cls)
    across = (z * ys + (ys - 1 - y), cls)
    other_x = (rot, (xs - 1 - x) * cores + core)
    mate = (rot, x * cores + (cores - 1 - core))
    UP, DOWN, ACROSS, OTHER, MATE = range(5)

    def send(shard, unit, dev, kind):
        piece(shard, unit, core, dev, kind).start()

    def sent(shard, unit, dev, kind):
        piece(shard, unit, core, dev, kind).wait_send()

    def to_chip(act, shard, j, j_is_far=False):
        if j < crossing:
            act(shard, unit_of(j), other_x, OTHER)
        if cores == 2:
            act(shard, unit_of(j), mate, MATE)

    def arrive(shard, unit, half):
        piece(shard, unit, half, mate, MATE).wait_recv()

    def when(cond, fn):
        pl.when(cond)(fn)

    def z_visit(d, j, sign, act, wait):
        shard = (z - sign * d) * ys + y
        exists = (z >= d) if sign > 0 else (z + d < zs)

        def visit():
            if wait:
                arrive(shard, unit_of(j), core)
            more = (z + 1 < zs) if sign > 0 else (z >= 1)
            if d < zs - 1:
                @pl.when(more)
                def _():
                    act(shard, unit_of(j), up if sign > 0 else down, UP if sign > 0 else DOWN)
            if ys == 2:
                act(shard, unit_of(j), across, ACROSS)
            to_chip(act, shard, j)
        when(exists, visit)

    def y_visit(d, j, sign, act, wait):
        shard = (z - sign * d) * ys + (ys - 1 - y)

        def visit():
            if wait:
                arrive(shard, unit_of(j), core)
            to_chip(act, shard, j)
        if d == 0:
            visit()
        else:
            when((z >= d) if sign > 0 else (z + d < zs), visit)

    def x_visit(d, j, sign, row, act, wait):
        shard = (z - sign * d) * ys + row
        unit = unit_of(units - 1 - j)

        def visit():
            if wait:
                arrive(shard, unit, core)
            if cores == 2:
                act(shard, unit, mate, MATE)
        if d == 0:
            visit()
        else:
            when((z >= d) if sign > 0 else (z + d < zs), visit)

    def first(j, act):
        @pl.when(z + 1 < zs)
        def _():
            act(rot, unit_of(j), up, UP)

        @pl.when(z >= 1)
        def _():
            act(rot, unit_of(j), down, DOWN)
        if ys == 2:
            act(rot, unit_of(j), across, ACROSS)

    def slot(r, j, act, wait):
        signs = (1, -1)
        if r == 0:
            first(j, act)
        if 1 <= r <= zs - 1:
            for sign in signs:
                z_visit(r, j, sign, act, wait)
        if 1 <= r <= zs and ys == 2:
            for sign in (signs if r > 1 else (1,)):
                y_visit(r - 1, j, sign, act, wait)
        if j < crossing:
            if 2 <= r <= zs:
                for sign in signs:
                    x_visit(r - 1, j, sign, y, act, wait)
            if 2 <= r <= zs + 1 and ys == 2:
                for sign in (signs if r > 2 else (1,)):
                    x_visit(r - 2, j, sign, ys - 1 - y, act, wait)

    own.wait()
    for j in range(through):
        slot(0, j, send, True)

    lane = lax.broadcasted_iota(jnp.int32, (parts, 128), 1)
    power = jnp.zeros((parts, 128), jnp.float32)
    for r in range(CYCLES):
        v = part_value(g, rot, r, step)
        power = jnp.where(lane == r, jnp.sum(v * v, axis=1, keepdims=True) / step, power)
    power = power[:, :CYCLES]
    eye = (lax.broadcasted_iota(jnp.int32, (parts, parts), 0)
           == lax.broadcasted_iota(jnp.int32, (parts, parts), 1))
    mic_row = jnp.broadcast_to(mic_ref[...].astype(jnp.float32), (parts, parts))
    mic_col = jnp.sum(jnp.where(eye, mic_row, 0.0), axis=1, keepdims=True)
    same = (mic_row == mic_col).astype(jnp.float32)
    mean = jnp.dot(same, power, precision=lax.Precision.HIGHEST,
                   preferred_element_type=jnp.float32)
    mean = mean / jnp.sum(same, axis=1, keepdims=True)
    ctf = ctf_ref[...]
    ctf_part = jnp.zeros((parts, CYCLES), jnp.float32)
    for m in range(ctf.shape[0]):
        ctf_part = jnp.where(mic_col == float(m), ctf[m:m + 1, :], ctf_part)
    factor = ctf_part * lax.rsqrt(mean + 1e-6)
    fac[rot] = jnp.concatenate([factor, jnp.zeros((parts, 128 - CYCLES), jnp.float32)], axis=1)

    for copy in ref_copies:
        copy.wait()

    def pad_block(i, carry):
        cols = pl.ds(pl.multiple_of(i * 1024, 1024), 1024)
        for c in range(classes):
            refs_p[c, 0:angles, cols] = refs_v[c, :, cols]
        return carry
    lax.fori_loop(0, feats // 1024, pad_block, 0)

    def fac_copy(d, shard):
        return pltpu.make_async_remote_copy(
            src_ref=fac.at[shard], dst_ref=fac.at[shard], send_sem=fac_send.at[d],
            recv_sem=fac_recv.at[shard], device_id=(lax.rem(rot + d, n_rot), cls),
            device_id_type=pl.DeviceIdType.MESH)
    for d in range(1, n_rot):
        fac_copy(d, rot).start()

    for r in range(1, zs + 2):
        for j in range(through):
            slot(r, j, send, True)

    if cores == 2:
        for d in range(1, n_rot):
            shard = lax.rem(rot + d, n_rot)
            for u in range(units):
                arrive(shard, u, 1 - core)
    for d in range(1, n_rot):
        fac_copy(d, lax.rem(rot + n_rot - d, n_rot)).wait_recv()

    total = n_rot * parts
    fac_t[...] = fac[...].reshape(total, 128).T
    rows = refs_p.shape[0] * refs_p.shape[1]
    acc[...] = jnp.zeros_like(acc)

    def cycle_block(i, carry):
        part_sum = None
        for k in range(4):
            r = i * 4 + k
            cols = pl.ds(pl.multiple_of(r * step, 128), step)
            dot = lax.dot_general(
                refs_p[:, :, cols].reshape(rows, step), g[:, :, cols].reshape(total, step),
                (((1,), (1,)), ((), ())), preferred_element_type=jnp.float32)
            dot = dot * fac_t[pl.ds(r, 1), :]
            part_sum = dot if part_sum is None else part_sum + dot
        acc[...] += part_sum
        return carry
    lax.fori_loop(0, CYCLES // 4, cycle_block, 0)

    score = acc[...].reshape(classes, refs_p.shape[1], total)
    angle = lax.broadcasted_iota(jnp.int32, score.shape, 1)
    local = jnp.max(jnp.where(angle < angles, score, LOW), axis=1)
    local = jnp.concatenate([local, jnp.full((128 - classes, total), LOW, jnp.float32)], axis=0)
    cs_tx[...] = local.T.reshape(n_rot, parts, 128)

    def score_copy(d, block, slot_):
        return pltpu.make_async_remote_copy(
            src_ref=cs_tx.at[block], dst_ref=cs_rx.at[slot_], send_sem=sc_send.at[d],
            recv_sem=sc_recv.at[slot_], device_id=(lax.rem(rot + d, n_rot), cls),
            device_id_type=pl.DeviceIdType.MESH)
    for d in range(1, n_rot):
        score_copy(d, lax.rem(rot + d, n_rot), rot).start()
    best = cs_tx[rot]
    for d in range(1, n_rot):
        src = lax.rem(rot + n_rot - d, n_rot)
        score_copy(d, rot, src).wait_recv()
        best = jnp.maximum(best, cs_rx[src])
    cls_out[...] = best[:, :classes]

    prior_row = jnp.broadcast_to(prior_ref[...], (parts, parts))
    prior_col = jnp.sum(jnp.where(eye, prior_row, 0), axis=1, keepdims=True)
    chosen = (prior_col == lane + cls * classes) & (lane < classes)
    top = jnp.max(best, axis=1, keepdims=True)
    earlier = jnp.max(jnp.where(chosen, best, LOW), axis=1, keepdims=True)
    bp[cls] = jnp.where(lane == 0, top, earlier)

    def bp_copy(d, slot_):
        return pltpu.make_async_remote_copy(
            src_ref=bp.at[slot_], dst_ref=bp.at[slot_], send_sem=bp_send.at[d],
            recv_sem=bp_recv.at[slot_], device_id=(rot, lax.rem(cls + d, n_cls)),
            device_id_type=pl.DeviceIdType.MESH)
    for d in range(1, n_cls):
        bp_copy(d, cls).start()
    both = bp[cls]
    for d in range(1, n_cls):
        src = lax.rem(cls + n_cls - d, n_cls)
        bp_copy(d, src).wait_recv()
        both = jnp.maximum(both, bp[src])
    best_out[...] = jnp.max(jnp.where(eye, both[:, 0:1], LOW), axis=0, keepdims=True)
    prior_out[...] = jnp.max(jnp.where(eye, both[:, 1:2], LOW), axis=0, keepdims=True)

    for r in range(zs + 2):
        for j in range(through):
            slot(r, j, sent, False)
    for d in range(1, n_rot):
        fac_copy(d, rot).wait_send()
        score_copy(d, rot, rot).wait_send()
    for d in range(1, n_cls):
        bp_copy(d, cls).wait_send()


def part_value(g, rot, r, step):
    return g[rot, :, r * step:(r + 1) * step].astype(jnp.float32)


def body(n_rot, n_cls, particles, references, micrograph, ctf, prior_class):
    parts, feats = particles.shape
    classes, angles, _ = references.shape
    padded = -(-angles // 16) * 16
    units = plan(n_rot, n_cls)[4]
    vmem = pl.BlockSpec(memory_space=pltpu.VMEM)
    hbm = pl.BlockSpec(memory_space=pl.ANY)
    dma = pltpu.SemaphoreType.DMA
    total = n_rot * parts
    out = pl.pallas_call(
        functools.partial(kernel, n_rot, n_cls),
        out_shape=(jax.ShapeDtypeStruct((parts, classes), jnp.float32),
                   jax.ShapeDtypeStruct((1, parts), jnp.float32),
                   jax.ShapeDtypeStruct((1, parts), jnp.float32)),
        in_specs=[hbm, hbm, vmem, vmem, vmem],
        out_specs=(vmem, vmem, vmem),
        scratch_shapes=[
            pltpu.VMEM((n_rot, parts, feats), jnp.bfloat16),
            pltpu.VMEM((classes, angles, feats), jnp.bfloat16),
            pltpu.VMEM((classes, padded, feats), jnp.bfloat16),
            pltpu.VMEM((classes * padded, total), jnp.float32),
            pltpu.VMEM((n_rot, parts, 128), jnp.float32),
            pltpu.VMEM((128, total), jnp.float32),
            pltpu.VMEM((n_rot, parts, 128), jnp.float32),
            pltpu.VMEM((n_rot, parts, 128), jnp.float32),
            pltpu.VMEM((n_cls, parts, 128), jnp.float32),
            dma, dma((classes,)), dma((n_rot, 2 * units)), dma((5, n_rot, units)),
            dma((n_rot,)), dma((n_rot,)), dma((n_rot,)), dma((n_rot,)),
            dma((n_cls,)), dma((n_cls,)),
        ],
        compiler_params=pltpu.CompilerParams(
            collective_id=0, has_side_effects=True, vmem_limit_bytes=VMEM_BYTES),
    )(particles, references, micrograph, ctf, prior_class.reshape(1, parts))
    return out[0], out[1].reshape(parts), out[2].reshape(parts)


def solution(mesh):
    in_specs = (P("rot", None), P("cls", "rot", None), P("rot", None), P("rot", None), P("rot"))
    out_specs = (P("rot", "cls"), P("rot"), P("rot"))
    fn = functools.partial(body, mesh.shape["rot"], mesh.shape["cls"])
    return jax.shard_map(fn, mesh=mesh, in_specs=in_specs, out_specs=out_specs, check_vma=False)
```

time: 119 us -> 48.3 us (0.41)
  waiting for transfers between devices: 75.4 us -> 0 us
  Pallas kernels: 0 us -> 43.8 us
  between operations: 14.2 us -> 0.64 us
  local copies, waits for them, and re-layouts: 9.95 us -> 3.61 us
  blocking collectives: 6.17 us -> 0 us
  matrix products: 5.32 us -> 0 us
  other arithmetic: 3.92 us -> 0 us
  starting transfers between devices: 3.37 us -> 0 us
    all_gather x1 -> x0, waiting for transfers between devices: 68.9 us -> none  [body(): portion = lax.all_gather(whitened, 'rot', axis=0, tiled=True)]
    pallas_call x0 -> x1, Pallas kernels: none -> 43.8 us  [body(): pl.pallas_call(functools.partial(kernel, n_rot, n_cls), out_shape=(jax.Sh...]
    reshape x4 -> x0, local copies, waits for them, and re-layouts: 6.82 us -> none  [the longest x1 6.73 us: body(): ref_table = references.reshape(class_count * angle_count, features)]
    all_to_all x1 -> x0, waiting for transfers between devices: 6.45 us -> none  [body(): lax.all_to_all(blocks, 'rot', split_axis=1, concat_axis=1, tiled=True)]
    pmax x1 -> x0, blocking collectives: 6.17 us -> none  [body(): best_score, prior_score = lax.pmax((local_best, local_prior), 'cls')]
    dot_general x3 -> x0, matrix products: 5.32 us -> none  [the longest x1 5 us: body(): lax.dot_general(ref_table, portion, (((1,), (1,)), ((), ())), preferred_e...]
    all_to_all x1 -> x0, starting transfers between devices: 3.33 us -> none  [body(): lax.all_to_all(blocks, 'rot', split_axis=1, concat_axis=1, tiled=True)]
    unnamed x13 -> x3, local copies, waits for them, and re-layouts: 2.4 us -> 3.61 us
  transfers between devices with their start and end apart: 2 -> 0, of which waited for: 2 -> 0; matrix products, arithmetic and copies ran while one was open for 6% -> 0% of each run, Pallas kernels for 0% -> 0%
where the time goes in v1:
time: 48.3 us; the launch traced here: 48.1 us
  Pallas kernels  43.8 us (91%)
  local copies, waits for them, and re-layouts  3.61 us (7%)
  between operations  0.64 us (1%)
    pallas_call x1, Pallas kernels, body(): pl.pallas_call(functools.partial(kernel, n_rot, n_cls), out_shape=(jax.Sh...  43.8 us
    unnamed x3, local copies, waits for them, and re-layouts  3.61 us

profile of v1, /device:TPU:0, one launch (start us, length us, event | category | flops | bytes accessed | tf_op | source)
XLA Modules:
  0.0 48.1 jit_solution(8041802817690566749)
XLA Ops:
  0.6 43.8 %shard_map.76 = (f32[16,12]{1,0:T(8,128)}, f32[1,16]{1,0:T(1,128)}, f32[1,16]{1,0:T(1,128)}) custom-call(bf16[16,16384]{1,0:T(8,128)(2,1)} %part_ref.1, bf16[12,12,16384]{2,1,0:T(8,128)(2,1)} %ref_ref.1, s32[1,16]{1,0:T(1,128)} %mic_ref.1, f32[4,64]{1,0:T(4,128)} %ctf_ref.1, s32[1,16]{1,0:T(1,128)} %bitcast.3), custom_call_target="tpu_custom_call" | custom-call | tf_op jit(solution)/shard_map/pallas_call | solution.py:302
  44.5 1.3 %copy.11 = f32[16,12]{1,0:T(8,128)} copy(f32[16,12]{1,0:T(8,128)} %get-tuple-element.12) | data formatting | bytes 1536
  45.7 1.1 %copy.12 = f32[16]{0:T(128)} copy(f32[16]{0:T(128)} %bitcast.5) | data formatting | bytes 128
  46.9 1.2 %copy.13 = f32[16]{0:T(128)} copy(f32[16]{0:T(128)} %bitcast.4) | data formatting | bytes 128

commit v2 on v1

v2 whole, which is shorter than its diff:
```python
import functools
import jax
import jax.numpy as jnp
from jax import lax
from jax.experimental import pallas as pl
from jax.experimental.pallas import tpu as pltpu
from jax.sharding import PartitionSpec as P

CYCLES = 64
LOW = -1e30
EDGE, MIDS = 6, 1
VMEM_BYTES = 62 * 1024 * 1024


def plan(n_rot, n_cls):
    ys = 2 if n_rot % 2 == 0 else 1
    cs = 2 if n_cls % 2 == 0 else 1
    half = CYCLES // cs
    if n_cls == 2 * cs and n_rot <= 16:
        edge = (EDGE * half) // 32
        mid = half - 4 * edge
        mids = [mid // MIDS] * MIDS
        widths, crossing = [edge, edge] + mids + [edge, edge], 2
    else:
        widths, crossing = [half], 0
    assert sum(widths) == half
    return n_rot // ys, ys, n_cls // cs, cs, widths, crossing


def kernel(n_rot, n_cls, part_ref, ref_ref, mic_ref, ctf_ref, prior_ref,
           res_out,
           g, refs_v, refs_p, acc, fac, fac_t, cs_tx, cs_rx, bp,
           own_sem, ref_sem, recv_sem, send_sem, fac_send, fac_recv,
           sc_send, sc_recv, bp_send, bp_recv):
    zs, ys, xs, cores, widths, crossing = plan(n_rot, n_cls)
    units = len(widths)
    through = units - crossing
    fac_at = min(2, through - 1)
    starts = [sum(widths[:u]) for u in range(units)]
    half_cycles = CYCLES // cores
    parts, feats = part_ref.shape
    classes, angles, _ = ref_ref.shape
    step = feats // CYCLES
    rot = lax.axis_index("rot")
    cls = lax.axis_index("cls")
    z, y = lax.div(rot, ys), lax.rem(rot, ys)
    x, core = lax.div(cls, cores), lax.rem(cls, cores)

    own = pltpu.make_async_copy(part_ref, g.at[rot], own_sem)
    own.start()
    ref_copies = [
        pltpu.make_async_copy(ref_ref.at[c], refs_v.at[c], ref_sem.at[c]) for c in range(classes)
    ]
    for copy in ref_copies:
        copy.start()

    up, down = ((z + 1) * ys + y, cls), ((z - 1) * ys + y, cls)
    across = (z * ys + (ys - 1 - y), cls)
    other_x = (rot, (xs - 1 - x) * cores + core)
    mate = (rot, x * cores + (cores - 1 - core))
    has_up, has_down = z + 1 < zs, z >= 1
    UP, DOWN, ACROSS, OTHER, MATE = range(5)

    barrier = pltpu.get_barrier_semaphore()

    def greet(dev):
        pl.semaphore_signal(barrier, inc=1, device_id=dev,
                            device_id_type=pl.DeviceIdType.MESH)
    near = ([across] if ys == 2 else []) + ([other_x] if crossing else [])
    near += [mate] if cores == 2 else []
    pl.when(has_up)(lambda: greet(up))
    pl.when(has_down)(lambda: greet(down))
    for dev in near:
        greet(dev)
    pl.semaphore_wait(
        barrier, len(near) + jnp.where(has_up, 1, 0) + jnp.where(has_down, 1, 0))

    def unit_of(j):
        return jnp.where(x == 0, j, units - 1 - j) if crossing else j

    def cycle_of(j, half):
        first_cycle = jnp.where(x == 0, starts[j], starts[units - 1 - j]) if crossing else starts[j]
        return half * half_cycles + first_cycle

    def piece(shard, j, half, dev, kind):
        col = pl.multiple_of(cycle_of(j, half) * step, step)
        ref = g.at[shard, :, pl.ds(col, widths[j] * step)]
        unit = unit_of(j)
        return pltpu.make_async_remote_copy(
            src_ref=ref, dst_ref=ref,
            send_sem=send_sem.at[kind, shard, unit],
            recv_sem=recv_sem.at[shard, half * units + unit],
            device_id=dev, device_id_type=pl.DeviceIdType.MESH)

    def fac_copy(shard, dev, kind):
        return pltpu.make_async_remote_copy(
            src_ref=fac.at[shard], dst_ref=fac.at[shard], send_sem=fac_send.at[kind, shard],
            recv_sem=fac_recv.at[shard], device_id=dev, device_id_type=pl.DeviceIdType.MESH)

    def send(shard, j, dev, kind):
        piece(shard, j, core, dev, kind).start()

    def sent(shard, j, dev, kind):
        piece(shard, j, core, dev, kind).wait_send()

    def send_fac(shard, dev, kind):
        fac_copy(shard, dev, kind).start()

    def sent_fac(shard, dev, kind):
        fac_copy(shard, dev, kind).wait_send()

    def to_chip(act, shard, j):
        if j < crossing:
            act(shard, j, other_x, OTHER)
        if cores == 2:
            act(shard, j, mate, MATE)

    def arrive(shard, j, half):
        piece(shard, j, half, mate, MATE).wait_recv()

    def z_visit(d, j, sign, act, wait):
        shard = (z - sign * d) * ys + y
        exists = (z >= d) if sign > 0 else (z + d < zs)

        def visit():
            if wait:
                arrive(shard, j, core)
            more, dev, kind = (has_up, up, UP) if sign > 0 else (has_down, down, DOWN)
            if d < zs - 1:
                pl.when(more)(lambda: act(shard, j, dev, kind))
            if ys == 2:
                act(shard, j, across, ACROSS)
            to_chip(act, shard, j)
            if j == fac_at:
                if wait:
                    fac_copy(shard, mate, 0).wait_recv()
                fac_act = send_fac if wait else sent_fac
                if d < zs - 1:
                    pl.when(more)(lambda: fac_act(shard, dev, kind))
                if ys == 2:
                    fac_act(shard, across, ACROSS)
        pl.when(exists)(visit)

    def y_visit(d, j, sign, act, wait):
        shard = (z - sign * d) * ys + (ys - 1 - y)

        def visit():
            if wait:
                arrive(shard, j, core)
            to_chip(act, shard, j)
            if j == fac_at and wait:
                fac_copy(shard, mate, 0).wait_recv()
        if d == 0:
            visit()
        else:
            pl.when((z >= d) if sign > 0 else (z + d < zs))(visit)

    def x_visit(d, j, sign, row, act, wait):
        shard = (z - sign * d) * ys + row
        far = units - 1 - j

        def visit():
            if wait:
                arrive(shard, far, core)
            if cores == 2:
                act(shard, far, mate, MATE)
        if d == 0:
            visit()
        else:
            pl.when((z >= d) if sign > 0 else (z + d < zs))(visit)

    def first(act_on):
        pl.when(has_up)(lambda: act_on(up, UP))
        pl.when(has_down)(lambda: act_on(down, DOWN))
        if ys == 2:
            act_on(across, ACROSS)

    def slot(r, j, act, wait):
        signs = (1, -1)
        if r == 0:
            first(lambda dev, kind: act(rot, j, dev, kind))
        if 1 <= r <= zs - 1:
            for sign in signs:
                z_visit(r, j, sign, act, wait)
        if 1 <= r <= zs and ys == 2:
            for sign in (signs if r > 1 else (1,)):
                y_visit(r - 1, j, sign, act, wait)
        if j < crossing:
            if 2 <= r <= zs:
                for sign in signs:
                    x_visit(r - 1, j, sign, y, act, wait)
            if 2 <= r <= zs + 1 and ys == 2:
                for sign in (signs if r > 2 else (1,)):
                    x_visit(r - 2, j, sign, ys - 1 - y, act, wait)

    own.wait()
    for j in range(min(2, through)):
        slot(0, j, send, True)

    lane = lax.broadcasted_iota(jnp.int32, (parts, 128), 1)
    power = jnp.zeros((parts, 128), jnp.float32)
    for r in range(CYCLES):
        v = part_value(g, rot, r, step)
        power = jnp.where(lane == r, jnp.sum(v * v, axis=1, keepdims=True) / step, power)
    power = power[:, :CYCLES]
    eye = (lax.broadcasted_iota(jnp.int32, (parts, parts), 0)
           == lax.broadcasted_iota(jnp.int32, (parts, parts), 1))
    mic_row = jnp.broadcast_to(mic_ref[...].astype(jnp.float32), (parts, parts))
    mic_col = jnp.sum(jnp.where(eye, mic_row, 0.0), axis=1, keepdims=True)
    same = (mic_row == mic_col).astype(jnp.float32)
    mean = jnp.dot(same, power, precision=lax.Precision.HIGHEST,
                   preferred_element_type=jnp.float32)
    mean = mean / jnp.sum(same, axis=1, keepdims=True)
    ctf = ctf_ref[...]
    ctf_part = jnp.zeros((parts, CYCLES), jnp.float32)
    for m in range(ctf.shape[0]):
        ctf_part = jnp.where(mic_col == float(m), ctf[m:m + 1, :], ctf_part)
    factor = ctf_part * lax.rsqrt(mean + 1e-6)
    fac[rot] = jnp.concatenate([factor, jnp.zeros((parts, 128 - CYCLES), jnp.float32)], axis=1)
    acc[...] = jnp.zeros_like(acc)
    for j in range(min(2, through), fac_at + 1):
        slot(0, j, send, True)
    first(lambda dev, kind: send_fac(rot, dev, kind))
    for j in range(fac_at + 1, through):
        slot(0, j, send, True)

    for copy in ref_copies:
        copy.wait()

    def pad_block(i, carry):
        cols = pl.ds(pl.multiple_of(i * 1024, 1024), 1024)
        for c in range(classes):
            refs_p[c, 0:angles, cols] = refs_v[c, :, cols]
        return carry
    lax.fori_loop(0, feats // 1024, pad_block, 0)

    for r in range(1, zs):
        for j in range(through):
            slot(r, j, send, True)

    total = n_rot * parts
    rows = refs_p.shape[0] * refs_p.shape[1]

    def cycles_dot(first_cycle, count):
        part_sum = None
        for k in range(count):
            r = first_cycle + k
            cols = pl.ds(pl.multiple_of(r * step, step), step)
            dot = lax.dot_general(
                refs_p[:, :, cols].reshape(rows, step), g[:, :, cols].reshape(total, step),
                (((1,), (1,)), ((), ())), preferred_element_type=jnp.float32)
            dot = dot * fac_t[pl.ds(r, 1), :]
            part_sum = dot if part_sum is None else part_sum + dot
        acc[...] += part_sum

    def compute(j, half):
        if widths[j] <= 8:
            cycles_dot(cycle_of(j, half), widths[j])
        else:
            lax.fori_loop(
                0, widths[j], lambda i, c: (cycles_dot(cycle_of(j, half) + i, 1), c)[1], 0)

    def mate_units(j):
        for d in range(1, n_rot):
            arrive(lax.rem(rot + d, n_rot), j, 1 - core)
        compute(j, 1 - core)

    for j in range(fac_at + 1):
        slot(zs, j, send, True)
    fac_t[...] = fac[...].reshape(total, 128).T
    for j in range(fac_at):
        compute(j, core)
    for j in range(fac_at + 1, through):
        slot(zs, j, send, True)
    for j in range(crossing):
        slot(zs + 1, j, send, True)
    for j in range(fac_at, through):
        compute(j, core)
    for j in range(crossing):
        compute(units - 1 - j, core)
    if cores == 2:
        for j in range(units):
            mate_units(j)

    score = acc[...].reshape(classes, refs_p.shape[1], total)
    angle = lax.broadcasted_iota(jnp.int32, score.shape, 1)
    local = jnp.max(jnp.where(angle < angles, score, LOW), axis=1)
    local = jnp.concatenate([local, jnp.full((128 - classes, total), LOW, jnp.float32)], axis=0)
    cs_tx[...] = local.T.reshape(n_rot, parts, 128)

    def score_copy(d, block, slot_):
        return pltpu.make_async_remote_copy(
            src_ref=cs_tx.at[block], dst_ref=cs_rx.at[slot_], send_sem=sc_send.at[d],
            recv_sem=sc_recv.at[slot_], device_id=(lax.rem(rot + d, n_rot), cls),
            device_id_type=pl.DeviceIdType.MESH)
    for d in range(1, n_rot):
        score_copy(d, lax.rem(rot + d, n_rot), rot).start()
    for r in range(zs + 2):
        for j in range(through):
            slot(r, j, sent, False)
    first(lambda dev, kind: sent_fac(rot, dev, kind))
    best = cs_tx[rot]
    for d in range(1, n_rot):
        src = lax.rem(rot + n_rot - d, n_rot)
        score_copy(d, rot, src).wait_recv()
        best = jnp.maximum(best, cs_rx[src])

    prior_row = jnp.broadcast_to(prior_ref[...], (parts, parts))
    prior_col = jnp.sum(jnp.where(eye, prior_row, 0), axis=1, keepdims=True)
    chosen = (prior_col == lane + cls * classes) & (lane < classes)
    top = jnp.max(best, axis=1, keepdims=True)
    earlier = jnp.max(jnp.where(chosen, best, LOW), axis=1, keepdims=True)
    bp[cls] = jnp.where(lane == 0, top, earlier)

    def bp_copy(d, slot_):
        return pltpu.make_async_remote_copy(
            src_ref=bp.at[slot_], dst_ref=bp.at[slot_], send_sem=bp_send.at[d],
            recv_sem=bp_recv.at[slot_], device_id=(rot, lax.rem(cls + d, n_cls)),
            device_id_type=pl.DeviceIdType.MESH)
    for d in range(1, n_cls):
        bp_copy(d, cls).start()
    both = bp[cls]
    for d in range(1, n_cls):
        src = lax.rem(cls + n_cls - d, n_cls)
        bp_copy(d, src).wait_recv()
        both = jnp.maximum(both, bp[src])
    res_out[...] = jnp.where(lane == 126, both[:, 0:1], jnp.where(lane == 127, both[:, 1:2], best))
    for d in range(1, n_rot):
        score_copy(d, rot, rot).wait_send()
    for d in range(1, n_cls):
        bp_copy(d, cls).wait_send()


def finish(res_ref, cls_out, best_out, prior_out):
    res = res_ref[...]
    parts, classes = cls_out.shape
    cls_out[...] = res[:, :classes]
    eye = (lax.broadcasted_iota(jnp.int32, (parts, parts), 0)
           == lax.broadcasted_iota(jnp.int32, (parts, parts), 1))
    best_out[...] = jnp.max(jnp.where(eye, res[:, 126:127], LOW), axis=0, keepdims=True)
    prior_out[...] = jnp.max(jnp.where(eye, res[:, 127:128], LOW), axis=0, keepdims=True)


def part_value(g, rot, r, step):
    return g[rot, :, r * step:(r + 1) * step].astype(jnp.float32)


def body(n_rot, n_cls, particles, references, micrograph, ctf, prior_class):
    parts, feats = particles.shape
    classes, angles, _ = references.shape
    padded = -(-angles // 16) * 16
    units = len(plan(n_rot, n_cls)[4])
    vmem = pl.BlockSpec(memory_space=pltpu.VMEM)
    hbm = pl.BlockSpec(memory_space=pl.ANY)
    dma = pltpu.SemaphoreType.DMA
    total = n_rot * parts
    res = pl.pallas_call(
        functools.partial(kernel, n_rot, n_cls),
        out_shape=jax.ShapeDtypeStruct((parts, 128), jnp.float32),
        in_specs=[hbm, hbm, vmem, vmem, vmem],
        out_specs=vmem,
        scratch_shapes=[
            pltpu.VMEM((n_rot, parts, feats), jnp.bfloat16),
            pltpu.VMEM((classes, angles, feats), jnp.bfloat16),
            pltpu.VMEM((classes, padded, feats), jnp.bfloat16),
            pltpu.VMEM((classes * padded, total), jnp.float32),
            pltpu.VMEM((n_rot, parts, 128), jnp.float32),
            pltpu.VMEM((128, total), jnp.float32),
            pltpu.VMEM((n_rot, parts, 128), jnp.float32),
            pltpu.VMEM((n_rot, parts, 128), jnp.float32),
            pltpu.VMEM((n_cls, parts, 128), jnp.float32),
            dma, dma((classes,)), dma((n_rot, 2 * units)), dma((5, n_rot, units)),
            dma((3, n_rot)), dma((n_rot,)), dma((n_rot,)), dma((n_rot,)),
            dma((n_cls,)), dma((n_cls,)),
        ],
        compiler_params=pltpu.CompilerParams(
            collective_id=0, has_side_effects=True, vmem_limit_bytes=VMEM_BYTES),
    )(particles, references, micrograph, ctf, prior_class.reshape(1, parts))
    out = pl.pallas_call(
        finish,
        out_shape=(jax.ShapeDtypeStruct((parts, classes), jnp.float32),
                   jax.ShapeDtypeStruct((1, parts), jnp.float32),
                   jax.ShapeDtypeStruct((1, parts), jnp.float32)),
        in_specs=[vmem], out_specs=(vmem, vmem, vmem),
    )(res)
    return out[0], out[1].reshape(parts), out[2].reshape(parts)


def solution(mesh):
    in_specs = (P("rot", None), P("cls", "rot", None), P("rot", None), P("rot", None), P("rot"))
    out_specs = (P("rot", "cls"), P("rot"), P("rot"))
    fn = functools.partial(body, mesh.shape["rot"], mesh.shape["cls"])
    return jax.shard_map(fn, mesh=mesh, in_specs=in_specs, out_specs=out_specs, check_vma=False)
```

time: 48.3 us -> 41.5 us (0.86)
  local copies, waits for them, and re-layouts: 3.61 us -> 0 us
  Pallas kernels: 43.8 us -> 40.6 us
    unnamed x3 -> x0, local copies, waits for them, and re-layouts: 3.61 us -> none
    pallas_call x1 -> x2, Pallas kernels: 43.8 us -> 40.6 us  [the longest x1 39.3 us: body(): pl.pallas_call(functools.partial(kernel, n_rot, n_cls), out_shape=jax.Sha...]
where the time goes in v2:
time: 41.5 us; the launch traced here: 41.2 us
  Pallas kernels  40.6 us (98%)
  between operations  0.64 us (2%)
    pallas_call x1, Pallas kernels, body(): pl.pallas_call(functools.partial(kernel, n_rot, n_cls), out_shape=jax.Sha...  39.3 us
    pallas_call x1, Pallas kernels, body(): pl.pallas_call(finish, out_shape=(jax.ShapeDtypeStruct((parts, classes),...  1.3 us

profile of v2, /device:TPU:0, one launch (start us, length us, event | category | flops | bytes accessed | tf_op | source)
XLA Modules:
  0.0 41.2 jit_solution(1049753559519267796)
XLA Ops:
  0.6 39.3 %shard_map.76.res_ref = f32[16,128]{1,0:T(8,128)} custom-call(bf16[16,16384]{1,0:T(8,128)(2,1)} %part_ref.1, bf16[12,12,16384]{2,1,0:T(8,128)(2,1)} %ref_ref.1, s32[1,16]{1,0:T(1,128)} %mic_ref.1, f32[4,64]{1,0:T(4,128)} %ctf_ref.1, s32[1,16]{1,0:T(1,128)} %bitcast.3), custom_call_target="tpu_custom_call" | custom-call | tf_op jit(solution)/shard_map/pallas_call | solution.py:357
  39.9 1.3 %shard_map.77 = (f32[16,12]{1,0:T(8,128)}, f32[1,16]{1,0:T(1,128)}, f32[1,16]{1,0:T(1,128)}) custom-call(f32[16,128]{1,0:T(8,128)} %shard_map.76.res_ref), custom_call_target="tpu_custom_call" | custom-call | tf_op jit(solution)/shard_map/pallas_call | solution.py:379

commit v3 on v2

--- a/solution.py
+++ b/solution.py
@@ -9,6 +9,7 @@
 CYCLES = 64
 LOW = -1e30
 EDGE, MIDS = 6, 1
+XLAG, YLAG = 2, 3
 VMEM_BYTES = 62 * 1024 * 1024
 
 
@@ -35,7 +36,7 @@
     zs, ys, xs, cores, widths, crossing = plan(n_rot, n_cls)
     units = len(widths)
     through = units - crossing
-    fac_at = min(2, through - 1)
+    fac_at = min(1, through - 1)
     starts = [sum(widths[:u]) for u in range(units)]
     half_cycles = CYCLES // cores
     parts, feats = part_ref.shape
@@ -59,6 +60,7 @@
     other_x = (rot, (xs - 1 - x) * cores + core)
     mate = (rot, x * cores + (cores - 1 - core))
     has_up, has_down = z + 1 < zs, z >= 1
+    at_end = (z == 0) | (z == zs - 1)
     UP, DOWN, ACROSS, OTHER, MATE = range(5)
 
     barrier = pltpu.get_barrier_semaphore()
@@ -141,7 +143,7 @@
                     fac_act(shard, across, ACROSS)
         pl.when(exists)(visit)
 
-    def y_visit(d, j, sign, act, wait):
+    def y_visit(d, j, sign, act, wait, where):
         shard = (z - sign * d) * ys + (ys - 1 - y)
 
         def visit():
@@ -153,7 +155,7 @@
         if d == 0:
             visit()
         else:
-            pl.when((z >= d) if sign > 0 else (z + d < zs))(visit)
+            pl.when(((z >= d) if sign > 0 else (z + d < zs)) & where)(visit)
 
     def x_visit(d, j, sign, row, act, wait):
         shard = (z - sign * d) * ys + row
@@ -182,16 +184,20 @@
         if 1 <= r <= zs - 1:
             for sign in signs:
                 z_visit(r, j, sign, act, wait)
-        if 1 <= r <= zs and ys == 2:
-            for sign in (signs if r > 1 else (1,)):
-                y_visit(r - 1, j, sign, act, wait)
+        if ys == 2:
+            for d in range(zs):
+                for sign in (signs if d else (1,)):
+                    if r == d + 1:
+                        y_visit(d, j, sign, act, wait, at_end if d else None)
+                    if r == d + 2 and 1 <= d <= zs - 2:
+                        y_visit(d, j, sign, act, wait, jnp.logical_not(at_end))
         if j < crossing:
-            if 2 <= r <= zs:
-                for sign in signs:
-                    x_visit(r - 1, j, sign, y, act, wait)
-            if 2 <= r <= zs + 1 and ys == 2:
-                for sign in (signs if r > 2 else (1,)):
-                    x_visit(r - 2, j, sign, ys - 1 - y, act, wait)
+            for d in range(zs):
+                for sign in (signs if d else (1,)):
+                    if d and r == d + XLAG:
+                        x_visit(d, j, sign, y, act, wait)
+                    if ys == 2 and r == min(d + YLAG, zs + 1):
+                        x_visit(d, j, sign, ys - 1 - y, act, wait)
 
     own.wait()
     for j in range(min(2, through)):
@@ -268,18 +274,22 @@
     for j in range(fac_at + 1):
         slot(zs, j, send, True)
     fac_t[...] = fac[...].reshape(total, 128).T
-    for j in range(fac_at):
+    early = fac_at + 1 if through > fac_at + 1 else 0
+    for j in range(early):
         compute(j, core)
+    if cores == 2 and early:
+        mate_units(0)
     for j in range(fac_at + 1, through):
         slot(zs, j, send, True)
     for j in range(crossing):
         slot(zs + 1, j, send, True)
-    for j in range(fac_at, through):
+    if cores == 2:
+        for j in range(min(early, 1), early):
+            mate_units(j)
+    for j in list(range(early, through)) + [units - 1 - j for j in range(crossing)]:
         compute(j, core)
-    for j in range(crossing):
-        compute(units - 1 - j, core)
     if cores == 2:
-        for j in range(units):
+        for j in range(early, units):
             mate_units(j)
 
     score = acc[...].reshape(classes, refs_p.shape[1], total)

time: 41.5 us -> 40.8 us (0.983)
  Pallas kernels: 40.6 us -> 40 us
    pallas_call x1, Pallas kernels: 39.3 us -> 38.7 us  [body(): pl.pallas_call(functools.partial(kernel, n_rot, n_cls), out_shape=jax.Sha...]
where the time goes in v3:
time: 40.8 us; the launch traced here: 40.6 us
  Pallas kernels  40 us (98%)
  between operations  0.64 us (2%)
    pallas_call x1, Pallas kernels, body(): pl.pallas_call(functools.partial(kernel, n_rot, n_cls), out_shape=jax.Sha...  38.7 us
    pallas_call x1, Pallas kernels, body(): pl.pallas_call(finish, out_shape=(jax.ShapeDtypeStruct((parts, classes),...  1.3 us

profile of v3, /device:TPU:0, one launch (start us, length us, event | category | flops | bytes accessed | tf_op | source)
XLA Modules:
  0.0 40.6 jit_solution(15783736489403551400)
XLA Ops:
  0.6 38.7 %shard_map.76.res_ref = f32[16,128]{1,0:T(8,128)} custom-call(bf16[16,16384]{1,0:T(8,128)(2,1)} %part_ref.1, bf16[12,12,16384]{2,1,0:T(8,128)(2,1)} %ref_ref.1, s32[1,16]{1,0:T(1,128)} %mic_ref.1, f32[4,64]{1,0:T(4,128)} %ctf_ref.1, s32[1,16]{1,0:T(1,128)} %bitcast.3), custom_call_target="tpu_custom_call" | custom-call | tf_op jit(solution)/shard_map/pallas_call | solution.py:367
  39.3 1.3 %shard_map.77 = (f32[16,12]{1,0:T(8,128)}, f32[1,16]{1,0:T(1,128)}, f32[1,16]{1,0:T(1,128)}) custom-call(f32[16,128]{1,0:T(8,128)} %shard_map.76.res_ref), custom_call_target="tpu_custom_call" | custom-call | tf_op jit(solution)/shard_map/pallas_call | solution.py:389

commit v4 on v3

--- a/solution.py
+++ b/solution.py
@@ -52,8 +52,6 @@
     ref_copies = [
         pltpu.make_async_copy(ref_ref.at[c], refs_v.at[c], ref_sem.at[c]) for c in range(classes)
     ]
-    for copy in ref_copies:
-        copy.start()
 
     up, down = ((z + 1) * ys + y, cls), ((z - 1) * ys + y, cls)
     across = (z * ys + (ys - 1 - y), cls)
@@ -74,6 +72,8 @@
     pl.when(has_down)(lambda: greet(down))
     for dev in near:
         greet(dev)
+    for copy in ref_copies:
+        copy.start()
     pl.semaphore_wait(
         barrier, len(near) + jnp.where(has_up, 1, 0) + jnp.where(has_down, 1, 0))
 

time: 40.8 us -> 39.4 us (0.966)
  Pallas kernels: 40 us -> 38.5 us
    pallas_call x1, Pallas kernels: 38.7 us -> 37.2 us  [body(): pl.pallas_call(functools.partial(kernel, n_rot, n_cls), out_shape=jax.Sha...]
where the time goes in v4:
time: 39.4 us; the launch traced here: 39.2 us
  Pallas kernels  38.5 us (98%)
  between operations  0.64 us (2%)
    pallas_call x1, Pallas kernels, body(): pl.pallas_call(functools.partial(kernel, n_rot, n_cls), out_shape=jax.Sha...  37.2 us
    pallas_call x1, Pallas kernels, body(): pl.pallas_call(finish, out_shape=(jax.ShapeDtypeStruct((parts, classes),...  1.3 us

profile of v4, /device:TPU:0, one launch (start us, length us, event | category | flops | bytes accessed | tf_op | source)
XLA Modules:
  0.0 39.2 jit_solution(9833551366501639267)
XLA Ops:
  0.6 37.2 %shard_map.76.res_ref = f32[16,128]{1,0:T(8,128)} custom-call(bf16[16,16384]{1,0:T(8,128)(2,1)} %part_ref.1, bf16[12,12,16384]{2,1,0:T(8,128)(2,1)} %ref_ref.1, s32[1,16]{1,0:T(1,128)} %mic_ref.1, f32[4,64]{1,0:T(4,128)} %ctf_ref.1, s32[1,16]{1,0:T(1,128)} %bitcast.3), custom_call_target="tpu_custom_call" | custom-call | tf_op jit(solution)/shard_map/pallas_call | solution.py:367
  37.9 1.3 %shard_map.77 = (f32[16,12]{1,0:T(8,128)}, f32[1,16]{1,0:T(1,128)}, f32[1,16]{1,0:T(1,128)}) custom-call(f32[16,128]{1,0:T(8,128)} %shard_map.76.res_ref), custom_call_target="tpu_custom_call" | custom-call | tf_op jit(solution)/shard_map/pallas_call | solution.py:389
